TPU v7x, 32 devices: a whole 2x2x4 slice. The times are simulated.
32 devices in a mesh: grp: 1, sp: 32 (over z, y, x, core), ch: 1.
Axes of the slice: x: 2, y: 2, z: 4, core: 2. Of those that a mesh axis runs over, the one named last changes fastest.
Arguments:
- latents: bfloat16 [131072, 1024], P(('grp', 'sp')), may hold values from -6 to 6
- spectrum: bfloat16 [16, 64, 128, 1024], P(None, None, 'sp', 'ch'), may hold values from -4 to 4
- w_value: bfloat16 [1024, 1024], P('sp', 'ch'), may hold values from -0.1875 to 0.1875
- w_gate: bfloat16 [1024, 1024], P('sp', 'ch'), may hold values from -0.1875 to 0.1875
- w_out: bfloat16 [1024, 1024], P('sp'), may hold values from -0.1875 to 0.1875
- embed_table: bfloat16 [1024, 32768], P(('sp', 'ch')), may hold values from -12 to 12
- prompt_ids: int32 [256], P('grp'), may hold values from 0 to 32767
- noise_step: int32 [1], P('grp'), may hold values from 0 to 999
Outputs:
- denoised: bfloat16 [131072, 1024], P(('grp', 'sp', 'ch'))
All inputs are finite; a program needn't handle non-finite values.
Results may differ from a plain program's by a relative error of at most 0.013.
Values may be sent and summed in bfloat16 or wider, within the bound.
No kernel may reach another device: no remote copies, remote signals or barrier semaphores. Data moves between devices by JAX's collectives and lax.ppermute only.
A program may use at most 128 MiB of HBM per device.

v0:
```python
import math
import jax
import jax.numpy as jnp
from jax import lax
from jax.sharding import PartitionSpec as P

TT = 16
HH = 64
WW = 128
C = 1024


def cas_table(length):
    position = jnp.arange(length, dtype=jnp.int32)
    product = position[:, None] * position[None, :] % length
    phase_angle = product.astype(jnp.float32) * (2.0 * math.pi / length)
    return ((jnp.cos(phase_angle) + jnp.sin(phase_angle)) / math.sqrt(length)).astype(jnp.bfloat16)


def step_embedding(noise_step, channel, channels):
    half_count = channels // 2
    lower_half = channel < half_count
    position = jnp.where(lower_half, channel, channel - half_count).astype(jnp.float32)
    frequency = jnp.exp(-math.log(10000.0) * position / half_count)
    phase_angle = noise_step[0].astype(jnp.float32) * frequency
    return jnp.where(lower_half, jnp.sin(phase_angle), jnp.cos(phase_angle))


def apply_table(form, table, operand):
    return jnp.einsum(form, table, operand, preferred_element_type=jnp.float32)


def local(latents, spectrum, w_value, w_gate, w_out, embed_table, prompt_ids, noise_step):
    row_count = latents.shape[0]
    chan_part = w_value.shape[1]
    full_value, full_gate, full_out = (
        lax.all_gather(w_value, "sp", axis=0, tiled=True),
        lax.all_gather(w_gate, "sp", axis=0, tiled=True),
        lax.all_gather(w_out, "sp", axis=0, tiled=True),
    )
    value_rows = jnp.dot(latents, full_value, preferred_element_type=jnp.float32).astype(
        jnp.bfloat16
    )
    gate_rows = jnp.dot(latents, full_gate, preferred_element_type=jnp.float32)
    cas_width = cas_table(WW)
    cas_height = cas_table(HH)
    cas_time = cas_table(TT)
    line_grid = value_rows.reshape(row_count // WW, WW, chan_part)
    width_spec = apply_table("kw,lwc->lkc", cas_width, line_grid).astype(jnp.bfloat16)
    pencil = lax.all_to_all(width_spec, "sp", split_axis=1, concat_axis=0, tiled=True)
    band_count = pencil.shape[1]
    pencil = pencil.reshape(TT, HH, band_count, chan_part)
    height_spec = apply_table("ah,thkc->takc", cas_height, pencil).astype(jnp.bfloat16)
    full_spec = apply_table("st,takc->sakc", cas_time, height_spec).astype(jnp.bfloat16)
    filtered = (full_spec.astype(jnp.float32) * spectrum.astype(jnp.float32)).astype(jnp.bfloat16)
    time_back = apply_table("ts,sakc->takc", cas_time, filtered).astype(jnp.bfloat16)
    height_back = apply_table("ha,takc->thkc", cas_height, time_back).astype(jnp.bfloat16)
    returned = lax.all_to_all(
        height_back.reshape(TT * HH, band_count, chan_part),
        "sp",
        split_axis=0,
        concat_axis=1,
        tiled=True,
    )
    mix_rows = apply_table("wk,lkc->lwc", cas_width, returned).reshape(row_count, chan_part)
    offset = lax.axis_index("ch") * chan_part
    local_pool = jnp.mean(jnp.take(embed_table, prompt_ids, axis=1).astype(jnp.float32), axis=1)
    pooled_all = lax.all_gather(local_pool, ("sp", "ch"), axis=0, tiled=True)
    pooled = lax.dynamic_slice_in_dim(pooled_all, offset, chan_part)
    channel = offset + jnp.arange(chan_part, dtype=jnp.int32)
    modulation = 1.0 + pooled + step_embedding(noise_step, channel, C)
    mixed_rows = (mix_rows * jax.nn.silu(gate_rows) * modulation[None, :]).astype(jnp.bfloat16)
    half_rows = row_count // lax.axis_size("ch")
    own_rows = lax.dynamic_slice_in_dim(full_out, offset, chan_part, 0)
    summed = lax.psum_scatter(
        jnp.dot(mixed_rows, own_rows, preferred_element_type=jnp.float32).astype(jnp.bfloat16),
        "ch",
        scatter_dimension=0,
        tiled=True,
    ).astype(jnp.float32)
    residual = lax.dynamic_slice_in_dim(latents, lax.axis_index("ch") * half_rows, half_rows, 0)
    return (residual.astype(jnp.float32) + summed).astype(jnp.bfloat16)


def solution(mesh):
    placed = (
        P(("grp", "sp"), None),
        P(None, None, "sp", "ch"),
        P("sp", "ch"),
        P("sp", "ch"),
        P("sp", None),
        P(("sp", "ch"), None),
        P("grp"),
        P("grp"),
    )
    return jax.shard_map(
        local, mesh=mesh, in_specs=placed, out_specs=P(("grp", "sp", "ch"), None), check_vma=False
    )
```

profile of v0, /device:TPU:0, one launch (start us, length us, event | category | flops | bytes accessed | tf_op | source)
XLA Modules:
  0.0 686.7 jit_solution(4367004813713135409)
XLA Ops:
  6.5 0.0 all-gather.4.cloned.1.call-start
  6.5 0.7 all-gather.4.cloned.1.call-update
  7.3 61.9 %all-gather.4.cloned.1.call-done = bf16[1024,1024]{1,0:T(8,128)(2,1)} async-done(((bf16[32,1024]{1,0:T(8,128)(2,1)}), bf16[1024,1024]{1,0:T(8,128)(2,1)}) %all-gather.4.cloned.1.call-update) | async-done | bytes 2097168 | tf_op jit(solution)/shard_map/all_gather | solution.py:37
  69.1 12.8 %convolution_convert_fusion = bf16[4096,1024]{1,0:T(8,128)(2,1)S(1)} fusion(bf16[4096,1024]{1,0:T(8,128)(2,1)} %param.8, bf16[1024,1024]{1,0:T(8,128)(2,1)} %all-gather.4.cloned.1.call-done), kind=kOutput, calls=%fused_computation.18 | convolution fusion | flops 8594128896 | bytes 18874368 | tf_op jit(solution)/shard_map/dot_general | solution.py:41
  82.0 5.1 convert_bitcast_fusion.2
  87.1 12.4 %copy.18 = bf16[32,128,1024]{2,0,1:T(8,128)(2,1)} copy(bf16[32,128,1024]{1,2,0:T(8,128)(2,1)} %convert_bitcast_fusion.2) | data formatting | bytes 16777216 | tf_op jit(solution)/shard_map/convert_element_type | solution.py:49
  99.5 187.2 %all_to_all.33 = bf16[32,128,1024]{2,0,1:T(8,128)(2,1)} all-to-all(bf16[32,128,1024]{2,0,1:T(8,128)(2,1)} %copy.18), channel_id=1, replica_groups=mesh['grp'=1,'sp'=32,'ch'=1] {'sp'}, dimensions={1} | all-to-all | bytes 16777216 | tf_op jit(solution)/shard_map/all_to_all | solution.py:50
  286.7 8.6 %copy.19 = bf16[32,32,4,1024]{3,1,0,2:T(8,128)(2,1)} copy(bf16[32,32,4,1024]{3,1,2,0:T(8,128)(2,1)} %bitcast.48) | data formatting | bytes 16777216 | tf_op jit(solution)/shard_map/all_to_all | solution.py:50
  295.4 9.1 %convert_bitcast_fusion.1 = bf16[16,64,4,1024]{3,1,2,0:T(8,128)(2,1)} fusion(bf16[16,64,4,1024]{3,1,0,2:T(8,128)(2,1)} %bitcast.49), kind=kOutput, calls=%fused_computation.16 | convolution fusion | flops 541134848 | bytes 16777216 | tf_op jit(solution)/shard_map/ah,thkc->takc/dot_general | solution.py:30
  304.4 26.6 %fusion.15 = bf16[16,64,4,1024]{3,0,2,1:T(8,128)(2,1)} fusion(bf16[16,64,4,1024]{3,2,1,0:T(4,128)(2,1)} %param.9, bf16[16,64,4,1024]{3,1,2,0:T(8,128)(2,1)} %convert_bitcast_fusion.1), kind=kOutput, calls=%fused_computation.19 | convolution fusion | flops 293609984 | bytes 25165824 | tf_op jit(solution)/shard_map/ts,sakc->takc/dot_general | solution.py:30
  331.1 17.6 %convert_bitcast_fusion = bf16[16,64,4,1024]{3,1,2,0:T(8,128)(2,1)} fusion(bf16[16,64,4,1024]{3,0,2,1:T(8,128)(2,1)} %fusion.15), kind=kOutput, calls=%fused_computation.14 | convolution fusion | flops 541134848 | bytes 16777216 | tf_op jit(solution)/shard_map/ha,takc->thkc/dot_general | solution.py:30
  348.7 8.6 %copy.24 = bf16[16,64,4,1024]{3,1,0,2:T(8,128)(2,1)} copy(bf16[16,64,4,1024]{3,1,2,0:T(8,128)(2,1)} %convert_bitcast_fusion) | data formatting | bytes 16777216 | tf_op jit(solution)/shard_map/convert_element_type | solution.py:57
  357.2 12.5 %copy.25 = bf16[1024,4,1024]{2,1,0:T(4,128)(2,1)} copy(bf16[1024,4,1024]{2,0,1:T(8,128)(2,1)} %bitcast.50) | data formatting | bytes 16777216 | tf_op jit(solution)/shard_map/reshape | solution.py:59
  369.8 0.0 copy-start
  369.8 3.8 all-to-all-start.1
  373.6 0.0 copy-start.1
  373.6 0.0 all-gather.6.cloned.1.call-start
  373.7 0.7 all-gather.6.cloned.1.call-update
  374.4 0.0 all-gather.8.cloned.1.call-start
  374.4 0.7 all-gather.8.cloned.1.call-update
  375.1 0.0 copy-done
  375.1 5.9 copy.28
  381.7 0.0 copy-done.1
  381.7 5.2 gather_fusion
  386.9 0.1 convert_reduce_fusion
  387.0 0.1 multiply_dynamic-update-slice_fusion
  387.2 210.4 %all-reduce = f32[1024]{0:T(1024)S(1)} all-reduce(f32[1024]{0:T(1024)S(1)} %multiply_dynamic-update-slice_fusion), channel_id=1, replica_groups=mesh['grp'=1,'sp'=32,'ch'=1] {'sp','ch'}, use_global_device_ids=true, to_apply=%add | all-reduce | flops 1024 | bytes 8192
  597.6 0.0 all-to-all-done.1
  597.6 9.6 %copy.26 = bf16[1024,4,1024]{2,0,1:T(8,128)(2,1)} copy(bf16[1024,4,1024]{2,1,0:T(4,128)(2,1)} %all-to-all-done.1) | data formatting | bytes 16777216 | tf_op jit(solution)/shard_map/all_to_all | solution.py:58
  607.2 12.2 %copy.27 = bf16[32,32,4,1024]{3,2,1,0:T(4,128)(2,1)} copy(bf16[32,32,4,1024]{3,0,1,2:T(8,128)(2,1)} %bitcast.51) | data formatting | bytes 16777216 | tf_op jit(solution)/shard_map/all_to_all | solution.py:58
  619.4 12.5 %all_to_all.30 = bf16[32,128,1024]{2,1,0:T(8,128)(2,1)} reshape(bf16[32,32,4,1024]{3,2,1,0:T(4,128)(2,1)} %copy.27) | data formatting | bytes 16777216 | tf_op jit(solution)/shard_map/all_to_all | solution.py:58
  631.9 11.7 %fusion.32 = f32[32,1024,128]{1,2,0:T(8,128)} fusion(bf16[32,128,1024]{2,1,0:T(8,128)(2,1)} %all_to_all.30), kind=kOutput, calls=%fused_computation.41 | convolution fusion | flops 1074020352 | bytes 25165824 | tf_op jit(solution)/shard_map/wk,lkc->lwc/dot_general | solution.py:30
  643.6 0.0 all-gather.6.cloned.1.call-done
  643.6 20.4 %fusion.1 = bf16[4096,1024]{1,0:T(8,128)(2,1)} fusion(f32[32,1024,128]{1,2,0:T(8,128)} %fusion.32, f32[1024]{0:T(1024)S(1)} %select_add_fusion, bf16[4096,1024]{1,0:T(8,128)(2,1)} %param.8, bf16[1024,1024]{1,0:T(8,128)(2,1)} %all-gather.6.cloned.1.call-done), kind=kOutput, calls=%fused_computation.3 | convolution fusion | flops 8619294720 | bytes 35655680 | tf_op jit(solution)/shard_map/dot_general | solution.py:44
  663.9 0.0 all-gather.8.cloned.1.call-done
  663.9 16.1 %add_convert_fusion = bf16[4096,1024]{1,0:T(8,128)(2,1)} fusion(bf16[4096,1024]{1,0:T(8,128)(2,1)} %param.8, bf16[4096,1024]{1,0:T(8,128)(2,1)} %fusion.1, bf16[1024,1024]{1,0:T(8,128)(2,1)} %all-gather.8.cloned.1.call-done), kind=kOutput, calls=%fused_computation.4 | convolution fusion | flops 8610906112 | bytes 27262976 | tf_op jit(solution)/shard_map/dot_general | solution.py:76
  (5 shorter events, 0.1 us)
Async XLA Ops:
  6.5 62.6 %all-gather.4.cloned.1.call-start = ((), (), s32[]{:S(2)}) async-start(), calls=%async_computation.2 | async-start | bytes 2162688 | tf_op jit(solution)/shard_map/all_gather | solution.py:37
  369.8 5.3 copy-start
  369.8 227.8 %all-to-all-start.1 = ((bf16[1024,4,1024]{2,1,0:T(4,128)(2,1)}), bf16[1024,4,1024]{2,1,0:T(4,128)(2,1)}, u32[]{:S(2)}, u32[]{:S(2)}) async-start(bf16[1024,4,1024]{2,1,0:T(4,128)(2,1)} %copy.25), calls=%async_computation.1 | async-start | bytes 16777216 | tf_op jit(solution)/shard_map/all_to_all | solution.py:58
  373.6 8.1 %copy-start.1 = (s32[256]{0:T(256)S(1)}, s32[256]{0:T(256)}, u32[]{:S(2)}) copy-start(s32[256]{0:T(256)} %param.14) | copy-start | bytes 3076
  373.6 270.0 %all-gather.6.cloned.1.call-start = ((), (), s32[]{:S(2)}) async-start(), calls=%async_computation.3 | async-start | bytes 2162688 | tf_op jit(solution)/shard_map/all_gather | solution.py:38
  374.4 289.6 %all-gather.8.cloned.1.call-start = ((), (), s32[]{:S(2)}) async-start(), calls=%async_computation.4 | async-start | bytes 2162688 | tf_op jit(solution)/shard_map/all_gather | solution.py:39
Sparse Core Ops, SparseCore 0:
  10.2 58.9 all-gather.3
  377.3 96.9 all-gather.5
  477.2 78.9 all-gather.7
where the time goes:
time: 695 us; the launch traced here: 687 us
  blocking collectives  398 us (57%)
  matrix products  119 us (17%)
  local copies, waits for them, and re-layouts  87.6 us (13%)
  waiting for transfers between devices  64 us (9%)
  between operations  14 us (2%)
    unnamed x1, blocking collectives  210 us
    all_to_all x1, blocking collectives, local(): lax.all_to_all(width_spec, 'sp', split_axis=1, concat_axis=0, tiled=True)  187 us
    dot_general x5, matrix products, apply_table(): return jnp.einsum(form, table, operand, preferred_element_type=jnp.float32)  70.1 us
    all_gather x1, waiting for transfers between devices, local(): lax.all_gather(w_value, 'sp', axis=0, tiled=True)  61.9 us
    all_to_all x3, local copies, waits for them, and re-layouts, local(): lax.all_to_all(height_back.reshape(TT * HH, band_count, chan_part), 'sp',...  34.3 us
    dot_general x1, matrix products, local(): gate_rows = jnp.dot(latents, full_gate, preferred_element_type=jnp.float32)  20.4 us
    dot_general x1, matrix products, local(): jnp.dot(mixed_rows, own_rows, preferred_element_type=jnp.float32)  16.1 us
  transfers between devices with their start and end apart: 4, of which 1 were waited for; matrix products, arithmetic and copies ran while one was open for 10% of the time, Pallas kernels for 0%

commit v1 on v0

--- a/solution.py
+++ b/solution.py
@@ -47,7 +47,10 @@
     cas_time = cas_table(TT)
     line_grid = value_rows.reshape(row_count // WW, WW, chan_part)
     width_spec = apply_table("kw,lwc->lkc", cas_width, line_grid).astype(jnp.bfloat16)
-    pencil = lax.all_to_all(width_spec, "sp", split_axis=1, concat_axis=0, tiled=True)
+    pencil = jnp.concatenate(
+        lax.all_to_all(jnp.stack(jnp.split(width_spec, lax.axis_size("sp"), axis=1)), "sp", 0, 0),
+        axis=0,
+    )
     band_count = pencil.shape[1]
     pencil = pencil.reshape(TT, HH, band_count, chan_part)
     height_spec = apply_table("ah,thkc->takc", cas_height, pencil).astype(jnp.bfloat16)

time: 695 us -> 672 us (0.967)
  local copies, waits for them, and re-layouts: 87.6 us -> 70.7 us
    convert_element_type x1 -> x0, local copies, waits for them, and re-layouts: 12.4 us -> none  [local(): apply_table('kw,lwc->lkc', cas_width, line_grid).astype(jnp.bfloat16)]
    all_to_all x1 -> x0, local copies, waits for them, and re-layouts: 8.64 us -> none  [local(): lax.all_to_all(width_spec, 'sp', split_axis=1, concat_axis=0, tiled=True)]
where the time goes in v1:
time: 672 us; the launch traced here: 664 us
  blocking collectives  397 us (59%)
  matrix products  113 us (17%)
  local copies, waits for them, and re-layouts  70.7 us (11%)
  waiting for transfers between devices  64 us (10%)
  between operations  14.2 us (2%)
    unnamed x1, blocking collectives  210 us
    all_to_all x1, blocking collectives, local(): lax.all_to_all(jnp.stack(jnp.split(width_spec, lax.axis_size('sp'), axis=...  187 us
    dot_general x5, matrix products, apply_table(): return jnp.einsum(form, table, operand, preferred_element_type=jnp.float32)  64.2 us
    all_gather x1, waiting for transfers between devices, local(): lax.all_gather(w_value, 'sp', axis=0, tiled=True)  61.9 us
    all_to_all x3, local copies, waits for them, and re-layouts, local(): lax.all_to_all(height_back.reshape(TT * HH, band_count, chan_part), 'sp',...  34.3 us
    dot_general x1, matrix products, local(): gate_rows = jnp.dot(latents, full_gate, preferred_element_type=jnp.float32)  20.4 us
    dot_general x1, matrix products, local(): jnp.dot(mixed_rows, own_rows, preferred_element_type=jnp.float32)  16.1 us
  transfers between devices with their start and end apart: 4, of which 1 were waited for; matrix products, arithmetic and copies ran while one was open for 10% of the time, Pallas kernels for 0%

profile of v1, /device:TPU:0, one launch (start us, length us, event | category | flops | bytes accessed | tf_op | source)
XLA Modules:
  0.0 663.8 jit_solution(13410024349637824087)
XLA Ops:
  6.5 0.7 all-gather.4.cloned.1.call-update
  7.3 61.9 %all-gather.4.cloned.1.call-done = bf16[1024,1024]{1,0:T(8,128)(2,1)} async-done(((bf16[32,1024]{1,0:T(8,128)(2,1)}), bf16[1024,1024]{1,0:T(8,128)(2,1)}) %all-gather.4.cloned.1.call-update) | async-done | bytes 2097168 | tf_op jit(solution)/shard_map/all_gather | solution.py:37
  69.1 12.8 %convolution_convert_fusion = bf16[4096,1024]{1,0:T(8,128)(2,1)S(1)} fusion(bf16[4096,1024]{1,0:T(8,128)(2,1)} %param.8, bf16[1024,1024]{1,0:T(8,128)(2,1)} %all-gather.4.cloned.1.call-done), kind=kOutput, calls=%fused_computation.18 | convolution fusion | flops 8594128896 | bytes 18874368 | tf_op jit(solution)/shard_map/dot_general | solution.py:41
  82.0 2.6 convert_bitcast_fusion.2
  84.6 0.2 fusion.50
  84.8 0.1 fusion.49
  84.9 0.2 fusion.48
  85.2 0.2 fusion.46
  85.4 0.1 fusion.45
  85.5 0.2 fusion.44
  85.6 0.1 fusion.43
  85.8 0.2 fusion.42
  86.0 0.2 fusion.40
  86.2 0.1 fusion.39
  86.3 0.2 fusion.38
  86.5 0.1 fusion.37
  86.6 0.2 fusion.36
  86.8 0.1 fusion.35
  86.9 0.2 fusion.34
  87.0 0.1 fusion.33
  87.1 0.2 fusion.32
  87.4 0.2 fusion.30
  87.6 0.1 fusion.29
  87.7 0.2 fusion.28
  88.0 0.2 fusion.26
  88.3 0.2 fusion.24
  88.5 0.2 fusion.22
  88.8 0.2 fusion.20
  89.0 186.9 %all_to_all.23 = bf16[32,32,4,1024]{3,2,1,0:T(4,128)(2,1)S(1)} all-to-all(bf16[32,32,4,1024]{3,2,1,0:T(4,128)(2,1)S(1)} %fusion.20), channel_id=1, replica_groups=mesh['grp'=1,'sp'=32,'ch'=1] {'sp'}, dimensions={0} | all-to-all | bytes 16777216 | tf_op jit(solution)/shard_map/all_to_all | solution.py:51
  275.9 5.7 convert_bitcast_fusion.1
  281.6 26.5 %fusion.15 = bf16[16,64,4,1024]{3,0,2,1:T(8,128)(2,1)} fusion(bf16[16,64,4,1024]{3,2,1,0:T(4,128)(2,1)} %param.9, bf16[16,64,4,1024]{3,1,2,0:T(8,128)(2,1)} %convert_bitcast_fusion.1), kind=kOutput, calls=%fused_computation.19 | convolution fusion | flops 293609984 | bytes 25165824 | tf_op jit(solution)/shard_map/ts,sakc->takc/dot_general | solution.py:30
  308.1 17.7 %convert_bitcast_fusion = bf16[16,64,4,1024]{3,1,2,0:T(8,128)(2,1)} fusion(bf16[16,64,4,1024]{3,0,2,1:T(8,128)(2,1)} %fusion.15), kind=kOutput, calls=%fused_computation.14 | convolution fusion | flops 541134848 | bytes 16777216 | tf_op jit(solution)/shard_map/ha,takc->thkc/dot_general | solution.py:30
  325.8 8.4 %copy.17 = bf16[16,64,4,1024]{3,1,0,2:T(8,128)(2,1)} copy(bf16[16,64,4,1024]{3,1,2,0:T(8,128)(2,1)} %convert_bitcast_fusion) | data formatting | bytes 16777216 | tf_op jit(solution)/shard_map/convert_element_type | solution.py:60
  334.3 12.5 %copy.18 = bf16[1024,4,1024]{2,1,0:T(4,128)(2,1)} copy(bf16[1024,4,1024]{2,0,1:T(8,128)(2,1)} %bitcast.174) | data formatting | bytes 16777216 | tf_op jit(solution)/shard_map/reshape | solution.py:62
  346.8 3.9 all-to-all-start.1
  350.7 0.7 all-gather.6.cloned.1.call-update
  351.5 0.7 all-gather.8.cloned.1.call-update
  352.2 6.0 copy.21
  358.9 5.2 gather_fusion
  364.1 0.1 convert_reduce_fusion
  364.2 0.1 multiply_dynamic-update-slice_fusion
  364.3 210.3 %all-reduce = f32[1024]{0:T(1024)S(1)} all-reduce(f32[1024]{0:T(1024)S(1)} %multiply_dynamic-update-slice_fusion), channel_id=1, replica_groups=mesh['grp'=1,'sp'=32,'ch'=1] {'sp','ch'}, use_global_device_ids=true, to_apply=%add | all-reduce | flops 1024 | bytes 8192
  574.7 9.6 %copy.19 = bf16[1024,4,1024]{2,0,1:T(8,128)(2,1)} copy(bf16[1024,4,1024]{2,1,0:T(4,128)(2,1)} %all-to-all-done.1) | data formatting | bytes 16777216 | tf_op jit(solution)/shard_map/all_to_all | solution.py:61
  584.3 12.2 %copy.20 = bf16[32,32,4,1024]{3,2,1,0:T(4,128)(2,1)} copy(bf16[32,32,4,1024]{3,0,1,2:T(8,128)(2,1)} %bitcast.175) | data formatting | bytes 16777216 | tf_op jit(solution)/shard_map/all_to_all | solution.py:61
  596.5 12.5 %all_to_all.20 = bf16[32,128,1024]{2,1,0:T(8,128)(2,1)} reshape(bf16[32,32,4,1024]{3,2,1,0:T(4,128)(2,1)} %copy.20) | data formatting | bytes 16777216 | tf_op jit(solution)/shard_map/all_to_all | solution.py:61
  608.9 11.7 %fusion.65 = f32[32,1024,128]{1,2,0:T(8,128)} fusion(bf16[32,128,1024]{2,1,0:T(8,128)(2,1)} %all_to_all.20), kind=kOutput, calls=%fused_computation.105 | convolution fusion | flops 1074020352 | bytes 25165824 | tf_op jit(solution)/shard_map/wk,lkc->lwc/dot_general | solution.py:30
  620.6 20.4 %fusion.1 = bf16[4096,1024]{1,0:T(8,128)(2,1)} fusion(f32[32,1024,128]{1,2,0:T(8,128)} %fusion.65, f32[1024]{0:T(1024)S(1)} %select_add_fusion, bf16[4096,1024]{1,0:T(8,128)(2,1)} %param.8, bf16[1024,1024]{1,0:T(8,128)(2,1)} %all-gather.6.cloned.1.call-done), kind=kOutput, calls=%fused_computation.3 | convolution fusion | flops 8619294720 | bytes 35655680 | tf_op jit(solution)/shard_map/dot_general | solution.py:44
  641.0 16.1 %add_convert_fusion = bf16[4096,1024]{1,0:T(8,128)(2,1)} fusion(bf16[4096,1024]{1,0:T(8,128)(2,1)} %param.8, bf16[4096,1024]{1,0:T(8,128)(2,1)} %fusion.1, bf16[1024,1024]{1,0:T(8,128)(2,1)} %all-gather.8.cloned.1.call-done), kind=kOutput, calls=%fused_computation.4 | convolution fusion | flops 8610906112 | bytes 27262976 | tf_op jit(solution)/shard_map/dot_general | solution.py:79
  (23 shorter events, 1.0 us)
Async XLA Ops:
  6.5 62.6 %all-gather.4.cloned.1.call-start = ((), (), s32[]{:S(2)}) async-start(), calls=%async_computation.2 | async-start | bytes 2162688 | tf_op jit(solution)/shard_map/all_gather | solution.py:37
  346.8 5.4 copy-start
  346.8 227.9 %all-to-all-start.1 = ((bf16[1024,4,1024]{2,1,0:T(4,128)(2,1)}), bf16[1024,4,1024]{2,1,0:T(4,128)(2,1)}, u32[]{:S(2)}, u32[]{:S(2)}) async-start(bf16[1024,4,1024]{2,1,0:T(4,128)(2,1)} %copy.18), calls=%async_computation.1 | async-start | bytes 16777216 | tf_op jit(solution)/shard_map/all_to_all | solution.py:61
  350.7 8.2 %copy-start.1 = (s32[256]{0:T(256)S(1)}, s32[256]{0:T(256)}, u32[]{:S(2)}) copy-start(s32[256]{0:T(256)} %param.14) | copy-start | bytes 3076
  350.7 269.9 %all-gather.6.cloned.1.call-start = ((), (), s32[]{:S(2)}) async-start(), calls=%async_computation.3 | async-start | bytes 2162688 | tf_op jit(solution)/shard_map/all_gather | solution.py:38
  351.5 289.5 %all-gather.8.cloned.1.call-start = ((), (), s32[]{:S(2)}) async-start(), calls=%async_computation.4 | async-start | bytes 2162688 | tf_op jit(solution)/shard_map/all_gather | solution.py:39
Sparse Core Ops, SparseCore 0:
  10.2 58.9 all-gather.3
  354.4 96.9 all-gather.5
  454.3 78.9 all-gather.7
